TPU v7x, 32 devices: a whole 2x2x4 slice. The times are simulated.
32 devices in a mesh: blk: 32 (over z, y, x, core).
Axes of the slice: x: 2, y: 2, z: 4, core: 2. Of those that a mesh axis runs over, the one named last changes fastest.
Arguments:
- x_points: bfloat16 [1024, 128], P('blk'), may hold values from -5.2 to 5.2, as said below
- y_points: bfloat16 [1024, 128], P('blk'), may hold values from -5.2 to 5.2, as said below
Outputs:
- x_scores: float32 [1024, 3], P('blk')
- y_scores: float32 [1024, 3], P('blk')
- mmd_stat: float32 [3], replicated
- hsic_stat: float32 [3], replicated
Inputs may be any that keep to these rules, and one draw needn't show every extreme that they name: `x_points`: every entry of the first sample lies within -5.2 and 5.2. `y_points`: every entry of the second sample lies within -5.2 and 5.2.
All inputs are finite; a program needn't handle non-finite values.
Results may differ from a plain program's by a relative error of at most 0.00035.
Values may be sent and summed in bfloat16 or wider, within the bound.
A program may use at most 64 MiB of HBM per device.

v0:
```python
import jax
import jax.numpy as jnp
from jax import lax
from jax.sharding import PartitionSpec as P

WIDTHS = (0.08, 0.16, 0.32)


def folded(array, axis, dim, absorb, carry):
    whole = jax.tree.map(lambda part: lax.all_gather(part, axis, axis=dim, tiled=True), array)
    return absorb(carry, whole, jnp.int32(0))


def kernels(left, right):
    products = jnp.dot(left, right.T, preferred_element_type=jnp.float32)
    left_sq = jnp.sum(jnp.square(left.astype(jnp.float32)), axis=1)
    right_sq = jnp.sum(jnp.square(right.astype(jnp.float32)), axis=1)
    distance = jnp.maximum(left_sq[:, None] + right_sq[None, :] - 2.0 * products, 0.0)
    factor = 1.0 / (2.0 * jnp.array(WIDTHS, jnp.float32) * left.shape[1])
    return jnp.exp(-factor[:, None, None] * distance[None])


def pair_sums(left_x, left_y, right_x, right_y, offdiag):
    same_x = kernels(left_x, right_x)
    same_y = kernels(left_y, right_y)
    cross_xy = kernels(left_x, right_y)
    cross_yx = kernels(left_y, right_x)
    hadamard = same_x * same_y
    masked_x = same_x * offdiag
    masked_y = same_y * offdiag
    row_sums = jnp.stack(
        [
            jnp.sum(masked_x, 2),
            jnp.sum(masked_y, 2),
            jnp.sum(cross_xy, 2),
            jnp.sum(cross_yx, 2),
            jnp.sum(hadamard, 2),
        ]
    )
    col_sums = jnp.stack(
        [
            jnp.sum(masked_x, 1),
            jnp.sum(masked_y, 1),
            jnp.sum(cross_yx, 1),
            jnp.sum(cross_xy, 1),
            jnp.sum(hadamard, 1),
        ]
    )
    return (row_sums, col_sums)


def shards(x_points, y_points):
    local_rows = x_points.shape[0]
    own_first = lax.axis_index("blk") * local_rows
    row_index = own_first + jnp.arange(local_rows, dtype=jnp.int32)

    def add_block(running, pieces, offset):
        col_index = offset + jnp.arange(pieces[0].shape[0], dtype=jnp.int32)
        offdiag = (row_index[:, None] != col_index[None, :]).astype(jnp.float32)
        row_sums, col_sums = pair_sums(x_points, y_points, pieces[0], pieces[1], offdiag)
        return running + row_sums

    sums = folded(
        (x_points, y_points), "blk", 0, add_block, jnp.zeros((5, 3, local_rows), jnp.float32)
    )
    sum_xx, sum_yy, sum_xy, sum_yx, sum_h = (sums[0], sums[1], sums[2], sums[3], sums[4])
    full_x = sum_xx + 1.0
    full_y = sum_yy + 1.0
    partials = jnp.stack(
        [
            jnp.sum(sum_xx, 1),
            jnp.sum(sum_yy, 1),
            jnp.sum(sum_xy, 1),
            jnp.sum(sum_h, 1),
            jnp.sum(full_x * full_y, 1),
            jnp.sum(full_x, 1),
            jnp.sum(full_y, 1),
        ]
    )
    totals = lax.psum(partials, "blk")
    count_all = jnp.float32(local_rows * lax.axis_size("blk"))
    mmd_stat = count_all * (
        (totals[0] + totals[1]) / (count_all * (count_all - 1.0))
        - 2.0 * totals[2] / (count_all * count_all)
    )
    hsic_stat = (
        totals[3] - 2.0 * totals[4] / count_all + totals[5] * totals[6] / (count_all * count_all)
    ) / count_all
    x_scores = (jnp.log(sum_xx) - jnp.log(sum_xy)).T
    y_scores = (jnp.log(sum_yy) - jnp.log(sum_yx)).T
    return (x_scores, y_scores, mmd_stat, hsic_stat)


def solution(mesh):
    placed = (P("blk", None), P("blk", None))
    return jax.shard_map(
        shards,
        mesh=mesh,
        in_specs=placed,
        out_specs=(P("blk", None), P("blk", None), P(), P()),
        check_vma=False,
    )
```

profile of v0, /device:TPU:0, one launch (start us, length us, event | category | flops | bytes accessed | tf_op | source)
XLA Modules:
  0.0 123.4 jit_solution(14137911467279880896)
XLA Ops:
  0.6 0.0 copy-start.1
  0.6 0.0 copy-start
  0.7 0.7 copy-done.1
  1.3 0.1 multiply_reduce_fusion.4
  1.4 0.0 copy-done
  1.4 0.1 multiply_reduce_fusion.3
  1.6 0.1 fusion.16
  1.6 44.0 %all_gather.6 = bf16[1024,128]{1,0:T(8,128)(2,1)S(1)} all-gather(bf16[32,128]{1,0:T(8,128)(2,1)S(1)} %copy-done.1), channel_id=1, replica_groups=mesh['blk'=32] {'blk'}, dimensions={0}, use_global_device_ids=true | all-gather | bytes 270336 | tf_op jit(solution)/shard_map/all_gather | solution.py:10
  45.6 0.2 multiply_reduce_fusion.1
  45.9 0.2 fusion.1
  46.1 0.2 fusion.7
  46.3 37.4 %all_gather.7 = bf16[1024,128]{1,0:T(8,128)(2,1)S(1)} all-gather(bf16[32,128]{1,0:T(8,128)(2,1)S(1)} %copy-done), channel_id=1, replica_groups=mesh['blk'=32] {'blk'}, dimensions={0}, use_global_device_ids=true | all-gather | bytes 270336 | tf_op jit(solution)/shard_map/all_gather | solution.py:10
  83.6 0.2 multiply_reduce_fusion
  83.8 0.2 fusion.3
  84.0 0.0 copy-start.2
  84.1 0.2 fusion.5
  84.3 0.4 copy-done.2
  84.7 0.5 fusion.14
  85.2 0.7 add_reduce_fusion
  86.0 37.0 %psum.7 = f32[7,3]{1,0:T(8,128)S(1)} all-reduce(f32[7,3]{1,0:T(8,128)S(1)} %stack.31), channel_id=1, replica_groups=mesh['blk'=32] {'blk'}, use_global_device_ids=true, to_apply=%region_15.0 | all-reduce | flops 21 | bytes 168 | tf_op jit(solution)/shard_map/psum | solution.py:80
  122.9 0.5 multiply_bitcast_fusion
  (2 shorter events, 0.0 us)
Async XLA Ops:
  0.6 0.7 copy-start.1
  0.6 0.8 copy-start
  84.0 0.7 copy-start.2
where the time goes:
time: 124 us; the launch traced here: 123 us
  blocking collectives  118 us (95%)
  other arithmetic  2.47 us (2%)
    all_gather x2, blocking collectives, folded(): lax.all_gather(part, axis, axis=dim, tiled=True)  81.3 us
    psum x1, blocking collectives, shards(): totals = lax.psum(partials, 'blk')  37 us

commit v1 on v0

v1 whole, which is shorter than its diff:
```python
import functools
import math

import jax
import jax.numpy as jnp
from jax import lax
from jax.experimental import pallas as pl
from jax.experimental.pallas import tpu as pltpu
from jax.sharding import PartitionSpec as P

WIDTHS = (0.08, 0.16, 0.32)
LANES = 128
STEP = 16
MESH = pl.DeviceIdType.MESH


def plane_size(count):
    size = math.isqrt(count)
    while size * size < count or count % size:
        size += 1
    return size


def lane_norms(points):
    squares = jnp.square(points.astype(jnp.float32))
    high = squares.astype(jnp.bfloat16)
    low = (squares - high.astype(jnp.float32)).astype(jnp.bfloat16)
    ones = jnp.ones((8, points.shape[1]), jnp.bfloat16)
    dims = (((1,), (1,)), ((), ()))
    return lax.dot_general(
        ones, high, dims, preferred_element_type=jnp.float32
    ) + lax.dot_general(ones, low, dims, preferred_element_type=jnp.float32)


def fold8(array):
    return jnp.sum(array.reshape(array.shape[0] // 8, 8, array.shape[1]), 0)


def powers(widest):
    middle = widest * widest
    return [middle * middle, middle, widest]


def kernel(
    plane,
    depth,
    x_hbm,
    y_hbm,
    x_out,
    y_out,
    mmd_out,
    hsic_out,
    rows,
    cols,
    parts,
    tots,
    turn,
    load_sem,
    row_send,
    row_recv,
    col_send,
    col_recv,
    part_send,
    part_recv,
    tot_send,
    tot_recv,
):
    length, dim = x_hbm.shape
    count = plane * depth * length
    tiles = plane * length // LANES
    chunks = depth * length // LANES
    per_tile = LANES // length
    me = lax.axis_index("blk")
    mine = lax.rem(me, plane)
    layer = me // plane

    loads = [
        pltpu.make_async_copy(source, buffer.at[slot, pl.ds(first, length)], load_sem.at[k])
        for k, (source, buffer, slot, first) in enumerate(
            [
                (x_hbm, rows, mine, 0),
                (y_hbm, rows, mine, length),
                (x_hbm, cols, layer, 0),
                (y_hbm, cols, layer, length),
            ]
        )
    ]
    for load in loads:
        load.start()

    plane_peers = [layer * plane + lax.rem(mine + k, plane) for k in range(1, plane)]
    depth_peers = [lax.rem(layer + k, depth) * plane + mine for k in range(1, depth)]

    barrier = pltpu.get_barrier_semaphore()
    for peer in depth_peers + plane_peers:
        pl.semaphore_signal(barrier, inc=1, device_id=(peer,), device_id_type=MESH)
    for load in loads:
        load.wait()
    pl.semaphore_wait(barrier, plane + depth - 2)

    def spread(buffer, slot, peers, send, recv):
        copies = []
        for k, peer in enumerate(peers):
            copy = pltpu.make_async_remote_copy(
                src_ref=buffer.at[slot],
                dst_ref=buffer.at[slot],
                send_sem=send.at[k],
                recv_sem=recv.at[k],
                device_id=(peer,),
                device_id_type=MESH,
            )
            copy.start()
            copies.append(copy)
        return copies

    col_copies = spread(cols, layer, depth_peers, col_send, col_recv)
    row_copies = spread(rows, mine, plane_peers, row_send, row_recv)
    for copy in row_copies:
        copy.wait_recv()
    for copy in col_copies:
        copy.wait_recv()

    scale = -math.log2(math.e) / (2.0 * WIDTHS[2] * dim)
    dims = (((1,), (1,)), ((), ()))

    def tile_sums(tile):
        blocks = pl.ds(tile * per_tile, per_tile)
        left_x = rows[blocks, :length].reshape(LANES, dim)
        left_y = rows[blocks, length:].reshape(LANES, dim)
        left = jnp.concatenate([left_x, left_y], 0)
        norms = lane_norms(left)
        left_sq_x, left_sq_y = norms[:1, :LANES], norms[:1, LANES:]
        row_index = (
            layer * (plane * length)
            + tile * LANES
            + lax.broadcasted_iota(jnp.int32, (STEP, LANES), 1)
        )

        def chunk_sums(chunk, sums):
            blocks = pl.ds(chunk * per_tile, per_tile)
            right_x = cols[blocks, :length].reshape(LANES, dim)
            right_y = cols[blocks, length:].reshape(LANES, dim)
            right = jnp.concatenate([right_x, right_y], 0)
            right_sq = jnp.sum(jnp.square(right.astype(jnp.float32)), 1, keepdims=True)
            products = lax.dot_general(
                right * jnp.bfloat16(-2.0), left, dims, preferred_element_type=jnp.float32
            )
            sums = list(sums)
            for first in range(0, LANES, STEP):
                inner = lax.broadcasted_iota(jnp.int32, (STEP, LANES), 0)
                col_index = (
                    (chunk * per_tile + first // length) * plane + mine
                ) * length + (inner + first % length)
                diagonal = row_index == col_index
                sq_x = right_sq[first : first + STEP]
                sq_y = right_sq[LANES + first : LANES + first + STEP]

                def widest(left_sq, right_sq, products):
                    distance = jnp.maximum(left_sq + right_sq + products, 0.0)
                    return jnp.exp2(distance * scale)

                top = products[first : first + STEP]
                bottom = products[LANES + first : LANES + first + STEP]
                same_x = widest(left_sq_x, sq_x, top[:, :LANES])
                same_y = widest(left_sq_y, sq_y, bottom[:, LANES:])
                cross_xy = widest(left_sq_x, sq_y, bottom[:, :LANES])
                cross_yx = widest(left_sq_y, sq_x, top[:, LANES:])
                hadamard = same_x * same_y
                same_x = jnp.where(diagonal, 0.0, same_x)
                same_y = jnp.where(diagonal, 0.0, same_y)
                terms = []
                for value in (same_x, same_y, hadamard, cross_xy, cross_yx):
                    terms += powers(value)
                sums = [a + fold8(b) for a, b in zip(sums, terms)]
            return tuple(sums)

        sums = tuple(jnp.zeros((8, LANES), jnp.float32) for _ in range(15))
        if chunks == 1:
            sums = chunk_sums(0, sums)
        else:
            sums = lax.fori_loop(0, chunks, chunk_sums, sums)
        order = [0, 1, 2, 3, 4, 5, 6, 7, 9, 10, 11, 12, 13, 14, 8]
        flat = [jnp.sum(sums[k], 0, keepdims=True) for k in order]
        flat.append(jnp.zeros((1, LANES), jnp.float32))
        parts[mine, tile] = jnp.concatenate(flat, 0)

    if tiles <= 2:
        for tile in range(tiles):
            tile_sums(tile)
    else:

        @pl.loop(0, tiles)
        def _(tile):
            tile_sums(tile)

    part_copies = spread(parts, mine, plane_peers, part_send, part_recv)
    for copy in part_copies:
        copy.wait_recv()

    def whole_sums(tile):
        total = parts[0, tile]
        for k in range(1, plane):
            total = total + parts[k, tile]
        return total[:8], total[8:]

    upper_total = jnp.zeros((8, LANES), jnp.float32)
    lower_total = jnp.zeros((8, LANES), jnp.float32)
    cross_total = jnp.zeros((8, LANES), jnp.float32)
    for tile in range(tiles):
        upper, lower = whole_sums(tile)
        upper_total += upper
        lower_total += lower
        cross_total += (upper + 1.0) * (pltpu.roll(upper, 5, 0) + 1.0)
    lane = lax.broadcasted_iota(jnp.int32, (8, LANES), 1)
    packed = jnp.where(
        lane == 0,
        jnp.sum(upper_total, 1, keepdims=True),
        jnp.where(
            lane == 1,
            jnp.sum(lower_total, 1, keepdims=True),
            jnp.sum(cross_total, 1, keepdims=True),
        ),
    )
    tots[layer] = packed
    tot_copies = spread(tots, layer, depth_peers, tot_send, tot_recv)

    upper, lower = whole_sums(mine // per_tile)
    scores = jnp.log(upper) - jnp.log(lower)
    turn[...] = jnp.concatenate([scores, jnp.zeros((LANES - 8, LANES), jnp.float32)], 0).T
    own = turn[pl.ds(pl.multiple_of(lax.rem(mine, per_tile) * length, length), length)]
    x_out[...] = own[:, :3]
    y_out[...] = pltpu.roll(own, LANES - 3, 1)[:, :3]

    for copy in tot_copies:
        copy.wait_recv()
    total = tots[0]
    for k in range(1, depth):
        total = total + tots[k]
    flat = jnp.concatenate([total, jnp.zeros((LANES - 8, LANES), jnp.float32)], 0).T
    upper, lower, cross = flat[0:1], flat[1:2], flat[2:3]
    paired = pltpu.roll(upper, LANES - 3, 1)
    narrow = pltpu.roll(upper, LANES - 6, 1)
    wide = pltpu.roll(lower, LANES - 4, 1)
    hadamard = jnp.where(lane[:1] < 2, narrow, wide)
    size = float(count)
    rows_all = jnp.float32(size)
    mmd = size * ((upper + paired) / (size * (size - 1.0)) - 2.0 * lower / (size * size))
    hsic = (
        hadamard
        - 2.0 * cross / size
        + (upper + rows_all) * (paired + rows_all) / (size * size)
    ) / size
    mmd_out[...] = mmd[:, :3]
    hsic_out[...] = hsic[:, :3]
    for copy in col_copies + row_copies + part_copies + tot_copies:
        copy.wait_send()


def shards(x_points, y_points):
    length, dim = x_points.shape
    count = lax.axis_size("blk")
    plane = plane_size(count)
    depth = count // plane
    tiles = plane * length // LANES
    dma = pltpu.SemaphoreType.DMA
    x_scores, y_scores, mmd, hsic = pl.pallas_call(
        functools.partial(kernel, plane, depth),
        out_shape=(
            jax.ShapeDtypeStruct((length, 3), jnp.float32),
            jax.ShapeDtypeStruct((length, 3), jnp.float32),
            jax.ShapeDtypeStruct((1, 3), jnp.float32),
            jax.ShapeDtypeStruct((1, 3), jnp.float32),
        ),
        in_specs=[pl.BlockSpec(memory_space=pl.ANY)] * 2,
        out_specs=(pl.BlockSpec(memory_space=pltpu.VMEM),) * 4,
        scratch_shapes=[
            pltpu.VMEM((plane, 2 * length, dim), jnp.bfloat16),
            pltpu.VMEM((depth, 2 * length, dim), jnp.bfloat16),
            pltpu.VMEM((plane, tiles, 16, LANES), jnp.float32),
            pltpu.VMEM((depth, 8, LANES), jnp.float32),
            pltpu.VMEM((LANES, LANES), jnp.float32),
            dma((4,)),
            dma((plane,)),
            dma((plane,)),
            dma((depth,)),
            dma((depth,)),
            dma((plane,)),
            dma((plane,)),
            dma((depth,)),
            dma((depth,)),
        ],
        compiler_params=pltpu.CompilerParams(collective_id=0, has_side_effects=True),
    )(x_points, y_points)
    return x_scores, y_scores, mmd[0], hsic[0]


def solution(mesh):
    placed = (P("blk", None), P("blk", None))
    return jax.shard_map(
        shards,
        mesh=mesh,
        in_specs=placed,
        out_specs=(P("blk", None), P("blk", None), P(), P()),
        check_vma=False,
    )
```

time: 124 us -> 22.8 us (0.18)
  blocking collectives: 118 us -> 0 us
  Pallas kernels: 0 us -> 18.6 us
  other arithmetic: 2.47 us -> 0 us
  local copies, waits for them, and re-layouts: 1.14 us -> 3.22 us
    all_gather x2 -> x0, blocking collectives: 81.3 us -> none  [folded(): lax.all_gather(part, axis, axis=dim, tiled=True)]
    psum x1 -> x0, blocking collectives: 37 us -> none  [shards(): totals = lax.psum(partials, 'blk')]
    pallas_call x0 -> x1, Pallas kernels: none -> 18.6 us  [shards(): pl.pallas_call(functools.partial(kernel, plane, depth), out_shape=(jax.Sh...]
    unnamed x6 -> x10, local copies, waits for them, and re-layouts: 1.12 us -> 3.22 us
    reduce_sum x6 -> x0, other arithmetic: 1.86 us -> none  [the longest x1 0.73 us: shards(): jnp.sum(full_y, 1)]
where the time goes in v1:
time: 22.8 us; the launch traced here: 22.4 us
  Pallas kernels  18.6 us (82%)
  local copies, waits for them, and re-layouts  3.22 us (14%)
  between operations  0.65 us (3%)
    pallas_call x1, Pallas kernels, shards(): pl.pallas_call(functools.partial(kernel, plane, depth), out_shape=(jax.Sh...  18.6 us
    unnamed x10, local copies, waits for them, and re-layouts  3.22 us

profile of v1, /device:TPU:0, one launch (start us, length us, event | category | flops | bytes accessed | tf_op | source)
XLA Modules:
  0.0 22.4 jit_solution(8580017086561529967)
XLA Ops:
  0.6 18.6 %shard_map.57 = (f32[32,3]{1,0:T(8,128)}, f32[32,3]{1,0:T(8,128)}, f32[1,3]{1,0:T(1,128)}, f32[1,3]{1,0:T(1,128)}) custom-call(bf16[32,128]{1,0:T(8,128)(2,1)} %x_hbm.1, bf16[32,128]{1,0:T(8,128)(2,1)} %y_hbm.1), custom_call_target="tpu_custom_call" | custom-call | tf_op jit(solution)/shard_map/pallas_call | solution.py:266
  19.2 0.0 copy-start
  19.2 1.4 %copy.6 = f32[32,3]{0,1:T(4,128)} copy(f32[32,3]{1,0:T(8,128)} %get-tuple-element.12) | data formatting | bytes 768
  20.6 0.0 copy-done
  20.6 0.0 copy-start.2
  20.6 0.7 %copy.7 = f32[32,3]{0,1:T(4,128)} copy(f32[32,3]{1,0:T(8,128)S(1)} %copy-done) | data formatting | bytes 768
  21.3 0.0 copy-done.2
  21.3 0.0 copy-start.1
  21.3 0.5 %copy.10 = f32[3]{0:T(128)} copy(f32[3]{0:T(128)S(1)} %bitcast.3) | data formatting | bytes 24
  21.8 0.2 copy-done.1
  21.9 0.5 %copy.11 = f32[3]{0:T(128)} copy(f32[3]{0:T(128)S(1)} %bitcast.2) | data formatting | bytes 24
Async XLA Ops:
  19.2 1.4 %copy-start = (f32[32,3]{1,0:T(8,128)S(1)}, f32[32,3]{1,0:T(8,128)}, u32[]{:S(2)}) copy-start(f32[32,3]{1,0:T(8,128)} %get-tuple-element.13) | copy-start | bytes 1156
  20.6 0.7 %copy-start.2 = (f32[1,3]{1,0:T(1,128)S(1)}, f32[1,3]{1,0:T(1,128)}, u32[]{:S(2)}) copy-start(f32[1,3]{1,0:T(1,128)} %get-tuple-element.10) | copy-start | bytes 40
  21.3 0.7 %copy-start.1 = (f32[1,3]{1,0:T(1,128)S(1)}, f32[1,3]{1,0:T(1,128)}, u32[]{:S(2)}) copy-start(f32[1,3]{1,0:T(1,128)} %get-tuple-element.11) | copy-start | bytes 40

commit v2 on v1

--- a/solution.py
+++ b/solution.py
@@ -36,6 +36,17 @@
     return jnp.sum(array.reshape(array.shape[0] // 8, 8, array.shape[1]), 0)
 
 
+def stack8(arrays):
+    row = lax.broadcasted_iota(jnp.int32, (8, LANES), 0)
+    for shift in (1, 2, 4):
+        even = (row & shift) == 0
+        arrays = [
+            jnp.where(even, a, b) + pltpu.roll(jnp.where(even, b, a), shift, 0)
+            for a, b in zip(arrays[::2], arrays[1::2])
+        ]
+    return arrays[0]
+
+
 def powers(widest):
     middle = widest * widest
     return [middle * middle, middle, widest]
@@ -46,15 +57,11 @@
     depth,
     x_hbm,
     y_hbm,
-    x_out,
-    y_out,
-    mmd_out,
-    hsic_out,
+    out,
     rows,
     cols,
     parts,
     tots,
-    turn,
     load_sem,
     row_send,
     row_recv,
@@ -180,9 +187,9 @@
         else:
             sums = lax.fori_loop(0, chunks, chunk_sums, sums)
         order = [0, 1, 2, 3, 4, 5, 6, 7, 9, 10, 11, 12, 13, 14, 8]
-        flat = [jnp.sum(sums[k], 0, keepdims=True) for k in order]
-        flat.append(jnp.zeros((1, LANES), jnp.float32))
-        parts[mine, tile] = jnp.concatenate(flat, 0)
+        flat = [sums[k] for k in order] + [jnp.zeros((8, LANES), jnp.float32)]
+        parts[mine, tile, :8] = stack8(flat[:8])
+        parts[mine, tile, 8:] = stack8(flat[8:])
 
     if tiles <= 2:
         for tile in range(tiles):
@@ -211,49 +218,53 @@
         upper_total += upper
         lower_total += lower
         cross_total += (upper + 1.0) * (pltpu.roll(upper, 5, 0) + 1.0)
+    row = lax.broadcasted_iota(jnp.int32, (8, LANES), 0)
     lane = lax.broadcasted_iota(jnp.int32, (8, LANES), 1)
-    packed = jnp.where(
-        lane == 0,
-        jnp.sum(upper_total, 1, keepdims=True),
-        jnp.where(
-            lane == 1,
-            jnp.sum(lower_total, 1, keepdims=True),
-            jnp.sum(cross_total, 1, keepdims=True),
-        ),
+
+    def along_lanes(array):
+        sums = jnp.where(row == lane, jnp.sum(array, 1, keepdims=True), 0.0)
+        return jnp.broadcast_to(jnp.sum(sums, 0, keepdims=True), (8, LANES))
+
+    upper = along_lanes(upper_total)
+    lower = along_lanes(lower_total)
+    cross = along_lanes(cross_total)
+    paired = pltpu.roll(upper, LANES - 3, 1)
+    hadamard = jnp.where(
+        lane < 2, pltpu.roll(upper, LANES - 6, 1), pltpu.roll(lower, LANES - 4, 1)
     )
-    tots[layer] = packed
+    size = float(count)
+    mmd = (upper + paired) * (1.0 / (size - 1.0)) - lower * (2.0 / size)
+    hsic = hadamard * (1.0 / size) - cross * (2.0 / (size * size))
+    tots[layer] = jnp.where(
+        row == 0, mmd, jnp.where(row == 1, hsic, jnp.where(row == 2, upper, paired))
+    )
     tot_copies = spread(tots, layer, depth_peers, tot_send, tot_recv)
 
     upper, lower = whole_sums(mine // per_tile)
     scores = jnp.log(upper) - jnp.log(lower)
-    turn[...] = jnp.concatenate([scores, jnp.zeros((LANES - 8, LANES), jnp.float32)], 0).T
-    own = turn[pl.ds(pl.multiple_of(lax.rem(mine, per_tile) * length, length), length)]
-    x_out[...] = own[:, :3]
-    y_out[...] = pltpu.roll(own, LANES - 3, 1)[:, :3]
+    turn = lax.rem(LANES - lax.rem(mine, per_tile) * length, LANES)
+    scores = pltpu.roll(scores, turn, 1)
 
     for copy in tot_copies:
         copy.wait_recv()
     total = tots[0]
     for k in range(1, depth):
         total = total + tots[k]
-    flat = jnp.concatenate([total, jnp.zeros((LANES - 8, LANES), jnp.float32)], 0).T
-    upper, lower, cross = flat[0:1], flat[1:2], flat[2:3]
-    paired = pltpu.roll(upper, LANES - 3, 1)
-    narrow = pltpu.roll(upper, LANES - 6, 1)
-    wide = pltpu.roll(lower, LANES - 4, 1)
-    hadamard = jnp.where(lane[:1] < 2, narrow, wide)
-    size = float(count)
-    rows_all = jnp.float32(size)
-    mmd = size * ((upper + paired) / (size * (size - 1.0)) - 2.0 * lower / (size * size))
-    hsic = (
-        hadamard
-        - 2.0 * cross / size
-        + (upper + rows_all) * (paired + rows_all) / (size * size)
-    ) / size
-    mmd_out[...] = mmd[:, :3]
-    hsic_out[...] = hsic[:, :3]
+    means = total * (1.0 / size) + 1.0
+    product = means[2:3] * means[3:4] * (1.0 / size)
+    out[...] = jnp.where(
+        row < 6, scores, jnp.where(row == 6, total[0:1], total[1:2] + product)
+    )
     for copy in col_copies + row_copies + part_copies + tot_copies:
         copy.wait_send()
+
+
+def unpack(packed, x_out, y_out, mmd_out, hsic_out):
+    length = x_out.shape[1]
+    x_out[...] = packed[0:3, :length]
+    y_out[...] = packed[3:6, :length]
+    mmd_out[...] = packed[6:7, :3]
+    hsic_out[...] = packed[7:8, :3]
 
 
 def shards(x_points, y_points):
@@ -263,22 +274,16 @@
     depth = count // plane
     tiles = plane * length // LANES
     dma = pltpu.SemaphoreType.DMA
-    x_scores, y_scores, mmd, hsic = pl.pallas_call(
+    packed = pl.pallas_call(
         functools.partial(kernel, plane, depth),
-        out_shape=(
-            jax.ShapeDtypeStruct((length, 3), jnp.float32),
-            jax.ShapeDtypeStruct((length, 3), jnp.float32),
-            jax.ShapeDtypeStruct((1, 3), jnp.float32),
-            jax.ShapeDtypeStruct((1, 3), jnp.float32),
-        ),
+        out_shape=jax.ShapeDtypeStruct((8, LANES), jnp.float32),
         in_specs=[pl.BlockSpec(memory_space=pl.ANY)] * 2,
-        out_specs=(pl.BlockSpec(memory_space=pltpu.VMEM),) * 4,
+        out_specs=pl.BlockSpec(memory_space=pltpu.VMEM),
         scratch_shapes=[
             pltpu.VMEM((plane, 2 * length, dim), jnp.bfloat16),
             pltpu.VMEM((depth, 2 * length, dim), jnp.bfloat16),
             pltpu.VMEM((plane, tiles, 16, LANES), jnp.float32),
             pltpu.VMEM((depth, 8, LANES), jnp.float32),
-            pltpu.VMEM((LANES, LANES), jnp.float32),
             dma((4,)),
             dma((plane,)),
             dma((plane,)),
@@ -291,7 +296,16 @@
         ],
         compiler_params=pltpu.CompilerParams(collective_id=0, has_side_effects=True),
     )(x_points, y_points)
-    return x_scores, y_scores, mmd[0], hsic[0]
+    x_scores, y_scores, mmd, hsic = pl.pallas_call(
+        unpack,
+        out_shape=(
+            jax.ShapeDtypeStruct((3, length), jnp.float32),
+            jax.ShapeDtypeStruct((3, length), jnp.float32),
+            jax.ShapeDtypeStruct((1, 3), jnp.float32),
+            jax.ShapeDtypeStruct((1, 3), jnp.float32),
+        ),
+    )(packed)
+    return x_scores.T, y_scores.T, mmd[0], hsic[0]
 
 
 def solution(mesh):

time: 22.8 us -> 20.7 us (0.908)
  local copies, waits for them, and re-layouts: 3.22 us -> 0 us
  Pallas kernels: 18.6 us -> 19.7 us
    unnamed x10 -> x0, local copies, waits for them, and re-layouts: 3.22 us -> none
    pallas_call x1 -> x2, Pallas kernels: 18.6 us -> 19.7 us  [the longest x1 18.5 us: shards(): pl.pallas_call(functools.partial(kernel, plane, depth), out_shape=jax.Sha...]
where the time goes in v2:
time: 20.7 us; the launch traced here: 20.4 us
  Pallas kernels  19.7 us (95%)
  between operations  0.64 us (3%)
    pallas_call x1, Pallas kernels, shards(): pl.pallas_call(functools.partial(kernel, plane, depth), out_shape=jax.Sha...  18.5 us
    pallas_call x1, Pallas kernels, shards(): pl.pallas_call(unpack, out_shape=(jax.ShapeDtypeStruct((3, length), jnp.f...  1.26 us

profile of v2, /device:TPU:0, one launch (start us, length us, event | category | flops | bytes accessed | tf_op | source)
XLA Modules:
  0.0 20.4 jit_solution(12263159727925393950)
XLA Ops:
  0.6 18.5 %shard_map.57.packed = f32[8,128]{1,0:T(8,128)} custom-call(bf16[32,128]{1,0:T(8,128)(2,1)} %x_hbm.1, bf16[32,128]{1,0:T(8,128)(2,1)} %y_hbm.1), custom_call_target="tpu_custom_call" | custom-call | tf_op jit(solution)/shard_map/pallas_call | solution.py:277
  19.1 1.3 %shard_map.58 = (f32[3,32]{1,0:T(4,128)}, f32[3,32]{1,0:T(4,128)}, f32[1,3]{1,0:T(1,128)}, f32[1,3]{1,0:T(1,128)}) custom-call(f32[8,128]{1,0:T(8,128)} %shard_map.57.packed), custom_call_target="tpu_custom_call" | custom-call | tf_op jit(solution)/shard_map/pallas_call | solution.py:299

commit v3 on v2

--- a/solution.py
+++ b/solution.py
@@ -19,6 +19,20 @@
     while size * size < count or count % size:
         size += 1
     return size
+
+
+def others(index, size):
+    if size & (size - 1):
+        return [lax.rem(index + k, size) for k in range(1, size)]
+    found = []
+    for k in range(size - 1, 0, -1):
+        other, bit = index, 1
+        while bit < size:
+            if k & bit:
+                other = other + bit - 2 * bit * lax.rem(index // bit, 2)
+            bit *= 2
+        found.append(other)
+    return found
 
 
 def lane_norms(points):
@@ -74,8 +88,8 @@
 ):
     length, dim = x_hbm.shape
     count = plane * depth * length
-    tiles = plane * length // LANES
-    chunks = depth * length // LANES
+    tiles = depth * length // LANES
+    chunks = plane * length // LANES
     per_tile = LANES // length
     me = lax.axis_index("blk")
     mine = lax.rem(me, plane)
@@ -85,18 +99,18 @@
         pltpu.make_async_copy(source, buffer.at[slot, pl.ds(first, length)], load_sem.at[k])
         for k, (source, buffer, slot, first) in enumerate(
             [
-                (x_hbm, rows, mine, 0),
-                (y_hbm, rows, mine, length),
-                (x_hbm, cols, layer, 0),
-                (y_hbm, cols, layer, length),
+                (x_hbm, rows, layer, 0),
+                (y_hbm, rows, layer, length),
+                (x_hbm, cols, mine, 0),
+                (y_hbm, cols, mine, length),
             ]
         )
     ]
     for load in loads:
         load.start()
 
-    plane_peers = [layer * plane + lax.rem(mine + k, plane) for k in range(1, plane)]
-    depth_peers = [lax.rem(layer + k, depth) * plane + mine for k in range(1, depth)]
+    plane_peers = [layer * plane + other for other in others(mine, plane)]
+    depth_peers = [other * plane + mine for other in others(layer, depth)]
 
     barrier = pltpu.get_barrier_semaphore()
     for peer in depth_peers + plane_peers:
@@ -120,11 +134,11 @@
             copies.append(copy)
         return copies
 
-    col_copies = spread(cols, layer, depth_peers, col_send, col_recv)
-    row_copies = spread(rows, mine, plane_peers, row_send, row_recv)
+    row_copies = spread(rows, layer, depth_peers, row_send, row_recv)
+    col_copies = spread(cols, mine, plane_peers, col_send, col_recv)
+    for copy in col_copies:
+        copy.wait_recv()
     for copy in row_copies:
-        copy.wait_recv()
-    for copy in col_copies:
         copy.wait_recv()
 
     scale = -math.log2(math.e) / (2.0 * WIDTHS[2] * dim)
@@ -137,11 +151,10 @@
         left = jnp.concatenate([left_x, left_y], 0)
         norms = lane_norms(left)
         left_sq_x, left_sq_y = norms[:1, :LANES], norms[:1, LANES:]
+        lane = lax.broadcasted_iota(jnp.int32, (STEP, LANES), 1)
         row_index = (
-            layer * (plane * length)
-            + tile * LANES
-            + lax.broadcasted_iota(jnp.int32, (STEP, LANES), 1)
-        )
+            (tile * per_tile + lane // length) * plane + mine
+        ) * length + lax.rem(lane, length)
 
         def chunk_sums(chunk, sums):
             blocks = pl.ds(chunk * per_tile, per_tile)
@@ -155,9 +168,7 @@
             sums = list(sums)
             for first in range(0, LANES, STEP):
                 inner = lax.broadcasted_iota(jnp.int32, (STEP, LANES), 0)
-                col_index = (
-                    (chunk * per_tile + first // length) * plane + mine
-                ) * length + (inner + first % length)
+                col_index = layer * (plane * length) + chunk * LANES + first + inner
                 diagonal = row_index == col_index
                 sq_x = right_sq[first : first + STEP]
                 sq_y = right_sq[LANES + first : LANES + first + STEP]
@@ -182,14 +193,15 @@
             return tuple(sums)
 
         sums = tuple(jnp.zeros((8, LANES), jnp.float32) for _ in range(15))
-        if chunks == 1:
-            sums = chunk_sums(0, sums)
+        if chunks <= 2:
+            for chunk in range(chunks):
+                sums = chunk_sums(chunk, sums)
         else:
             sums = lax.fori_loop(0, chunks, chunk_sums, sums)
         order = [0, 1, 2, 3, 4, 5, 6, 7, 9, 10, 11, 12, 13, 14, 8]
         flat = [sums[k] for k in order] + [jnp.zeros((8, LANES), jnp.float32)]
-        parts[mine, tile, :8] = stack8(flat[:8])
-        parts[mine, tile, 8:] = stack8(flat[8:])
+        parts[layer, tile, :8] = stack8(flat[:8])
+        parts[layer, tile, 8:] = stack8(flat[8:])
 
     if tiles <= 2:
         for tile in range(tiles):
@@ -200,13 +212,13 @@
         def _(tile):
             tile_sums(tile)
 
-    part_copies = spread(parts, mine, plane_peers, part_send, part_recv)
+    part_copies = spread(parts, layer, depth_peers, part_send, part_recv)
     for copy in part_copies:
         copy.wait_recv()
 
     def whole_sums(tile):
         total = parts[0, tile]
-        for k in range(1, plane):
+        for k in range(1, depth):
             total = total + parts[k, tile]
         return total[:8], total[8:]
 
@@ -235,20 +247,20 @@
     size = float(count)
     mmd = (upper + paired) * (1.0 / (size - 1.0)) - lower * (2.0 / size)
     hsic = hadamard * (1.0 / size) - cross * (2.0 / (size * size))
-    tots[layer] = jnp.where(
+    tots[mine] = jnp.where(
         row == 0, mmd, jnp.where(row == 1, hsic, jnp.where(row == 2, upper, paired))
     )
-    tot_copies = spread(tots, layer, depth_peers, tot_send, tot_recv)
-
-    upper, lower = whole_sums(mine // per_tile)
+    tot_copies = spread(tots, mine, plane_peers, tot_send, tot_recv)
+
+    upper, lower = whole_sums(layer // per_tile)
     scores = jnp.log(upper) - jnp.log(lower)
-    turn = lax.rem(LANES - lax.rem(mine, per_tile) * length, LANES)
+    turn = lax.rem(LANES - lax.rem(layer, per_tile) * length, LANES)
     scores = pltpu.roll(scores, turn, 1)
 
     for copy in tot_copies:
         copy.wait_recv()
     total = tots[0]
-    for k in range(1, depth):
+    for k in range(1, plane):
         total = total + tots[k]
     means = total * (1.0 / size) + 1.0
     product = means[2:3] * means[3:4] * (1.0 / size)
@@ -272,39 +284,40 @@
     count = lax.axis_size("blk")
     plane = plane_size(count)
     depth = count // plane
-    tiles = plane * length // LANES
+    tiles = depth * length // LANES
     dma = pltpu.SemaphoreType.DMA
     packed = pl.pallas_call(
         functools.partial(kernel, plane, depth),
-        out_shape=jax.ShapeDtypeStruct((8, LANES), jnp.float32),
+        out_shape=pltpu.VMEM((8, LANES), jnp.float32),
         in_specs=[pl.BlockSpec(memory_space=pl.ANY)] * 2,
         out_specs=pl.BlockSpec(memory_space=pltpu.VMEM),
         scratch_shapes=[
+            pltpu.VMEM((depth, 2 * length, dim), jnp.bfloat16),
             pltpu.VMEM((plane, 2 * length, dim), jnp.bfloat16),
-            pltpu.VMEM((depth, 2 * length, dim), jnp.bfloat16),
-            pltpu.VMEM((plane, tiles, 16, LANES), jnp.float32),
-            pltpu.VMEM((depth, 8, LANES), jnp.float32),
+            pltpu.VMEM((depth, tiles, 16, LANES), jnp.float32),
+            pltpu.VMEM((plane, 8, LANES), jnp.float32),
             dma((4,)),
+            dma((depth,)),
+            dma((depth,)),
             dma((plane,)),
             dma((plane,)),
             dma((depth,)),
             dma((depth,)),
             dma((plane,)),
             dma((plane,)),
-            dma((depth,)),
-            dma((depth,)),
         ],
         compiler_params=pltpu.CompilerParams(collective_id=0, has_side_effects=True),
     )(x_points, y_points)
     x_scores, y_scores, mmd, hsic = pl.pallas_call(
         unpack,
+        in_specs=[pl.BlockSpec(memory_space=pltpu.VMEM)],
         out_shape=(
             jax.ShapeDtypeStruct((3, length), jnp.float32),
             jax.ShapeDtypeStruct((3, length), jnp.float32),
             jax.ShapeDtypeStruct((1, 3), jnp.float32),
             jax.ShapeDtypeStruct((1, 3), jnp.float32),
         ),
-    )(packed)
+    )(pltpu.with_memory_space_constraint(packed, pltpu.VMEM))
     return x_scores.T, y_scores.T, mmd[0], hsic[0]
 
 

time: 20.7 us -> 18.9 us (0.913)
  Pallas kernels: 19.7 us -> 18.1 us
    pallas_call x2, Pallas kernels: 19.7 us -> 18.1 us  [the longest x1 17.5 us: shards(): pl.pallas_call(functools.partial(kernel, plane, depth), out_shape=pltpu.V...]
where the time goes in v3:
time: 18.9 us; the launch traced here: 18.7 us
  Pallas kernels  18.1 us (96%)
  between operations  0.64 us (3%)
    pallas_call x1, Pallas kernels, shards(): pl.pallas_call(functools.partial(kernel, plane, depth), out_shape=pltpu.V...  17.5 us
    pallas_call x1, Pallas kernels, shards(): pl.pallas_call(unpack, in_specs=[pl.BlockSpec(memory_space=pltpu.VMEM)],...  0.59 us

profile of v3, /device:TPU:0, one launch (start us, length us, event | category | flops | bytes accessed | tf_op | source)
XLA Modules:
  0.0 18.7 jit_solution(16494426996704132546)
XLA Ops:
  0.6 17.5 %shard_map.57.packed = f32[8,128]{1,0:T(8,128)S(1)} custom-call(bf16[32,128]{1,0:T(8,128)(2,1)} %x_hbm.1, bf16[32,128]{1,0:T(8,128)(2,1)} %y_hbm.1), custom_call_target="tpu_custom_call" | custom-call | tf_op jit(solution)/shard_map/pallas_call | solution.py:289
  18.1 0.6 %shard_map.58 = (f32[3,32]{1,0:T(4,128)}, f32[3,32]{1,0:T(4,128)}, f32[1,3]{1,0:T(1,128)}, f32[1,3]{1,0:T(1,128)}) custom-call(f32[8,128]{1,0:T(8,128)S(1)} %shard_map.57.packed), custom_call_target="tpu_custom_call" | custom-call | tf_op jit(solution)/shard_map/pallas_call | solution.py:311
